TPU v7x, 32 devices: a whole 2x2x4 slice. The times are simulated.
32 devices in a mesh: row: 4 (over z), col: 8 (over y, x, core).
Axes of the slice: x: 2, y: 2, z: 4, core: 2. Of those that a mesh axis runs over, the one named last changes fastest.
Arguments:
- rho_real: float32 [4096, 4096], P('row', 'col'), may hold values from -2.5 to 4, as said below
- rho_imag: float32 [4096, 4096], P('row', 'col'), may hold values from -2.5 to 2.5, as said below
- hamiltonian: bfloat16 [4096, 4096], P('row', 'col'), may hold values from -1 to 1
- amplitudes: float32 [8, 4096], replicated, may hold values from 0.15 to 0.6
- offsets: int32 [8], replicated, may hold values from -16 to 16
- active_jumps: int32 [1], replicated, may hold values from 4 to 8
Outputs:
- rho_next_real: float32 [4096, 4096], P('row', 'col')
- rho_next_imag: float32 [4096, 4096], P('row', 'col')
Inputs may be any that keep to these rules, and one draw needn't show every extreme that they name: `rho_real`: symmetric, with every diagonal entry 0.5 or more. `rho_imag`: antisymmetric.
All inputs are finite; a program needn't handle non-finite values.
Results may differ from a plain program's by a relative error of at most 0.001.
Values may be sent and summed in bfloat16 or wider, within the bound.
A program may use at most 192 MiB of HBM per device.

v0:
```python
import jax
import jax.numpy as jnp
from jax import lax
from jax.sharding import PartitionSpec as P

OMAX = 16
step_size = 0.25


def extended(cells, sides, width):
    for axis, dim in sides:
        count = lax.axis_size(axis)
        ends = count - 1
        head = lax.slice_in_dim(cells, 0, width, axis=dim)
        tail = lax.slice_in_dim(cells, cells.shape[dim] - width, cells.shape[dim], axis=dim)
        cells = jnp.concatenate(
            [
                lax.ppermute(tail, axis, [(i, (i + 1) % count) for i in range(ends)]),
                cells,
                lax.ppermute(head, axis, [((i + 1) % count, i) for i in range(ends)]),
            ],
            axis=dim,
        )
    return cells


def dissipate(matrix, padded, amplitudes, offsets, active, row_first, col_first):
    height = matrix.shape[1]
    breadth = matrix.shape[2]
    levels = amplitudes.shape[1]
    margin = (padded.shape[1] - height) // 2
    positions = jnp.arange(levels, dtype=jnp.int32)
    summed = jnp.zeros(matrix.shape, matrix.dtype)
    for jump_slot in range(amplitudes.shape[0]):
        offset = offsets[jump_slot]
        inside = (positions + offset >= 0) & (positions + offset < levels)
        strength = jnp.where(inside, amplitudes[jump_slot], 0.0)
        outflow = jnp.pad(strength * strength, (margin, margin))
        outflow = lax.dynamic_slice_in_dim(outflow, margin - offset, levels)
        row_strength = lax.dynamic_slice_in_dim(strength, row_first, height)
        col_strength = lax.dynamic_slice_in_dim(strength, col_first, breadth)
        row_outflow = lax.dynamic_slice_in_dim(outflow, row_first, height)
        col_outflow = lax.dynamic_slice_in_dim(outflow, col_first, breadth)
        corner = margin + offset
        shifted = lax.dynamic_slice(padded, (jnp.int32(0), corner, corner), (2, height, breadth))
        contribution = (
            row_strength[:, None] * col_strength[None, :] * shifted
            - 0.5 * (row_outflow[:, None] + col_outflow[None, :]) * matrix
        )
        summed = summed + jnp.where(jump_slot < active, contribution, 0.0)
    return summed


def diagonal_sum(matrix, row_first, col_first):
    row_index = lax.broadcasted_iota(jnp.int32, matrix.shape, 0) + row_first
    col_index = lax.broadcasted_iota(jnp.int32, matrix.shape, 1) + col_first
    return jnp.sum(jnp.where(row_index == col_index, matrix, 0.0))


def local(rho_real, rho_imag, hamiltonian, amplitudes, offsets, active_jumps):
    height, breadth = rho_real.shape
    levels = amplitudes.shape[1]
    row_first = lax.axis_index("row") * height
    col_first = lax.axis_index("col") * breadth
    active = active_jumps[0]
    ham_columns = lax.all_gather(hamiltonian, "row", axis=0, tiled=True)
    start_trace = lax.psum(diagonal_sum(rho_real, row_first, col_first), ("row", "col"))

    def drift(real_part, imag_part):
        real_low = real_part.astype(jnp.bfloat16)
        imag_low = imag_part.astype(jnp.bfloat16)
        row_panel = lax.all_gather(hamiltonian, "col", axis=1, tiled=True)
        pieces = (
            lax.all_gather(real_low, "row", axis=0, tiled=True),
            lax.all_gather(imag_low, "row", axis=0, tiled=True),
        )
        strip = row_panel
        left_real = jnp.dot(strip, pieces[0], preferred_element_type=jnp.float32)
        left_imag = jnp.dot(strip, pieces[1], preferred_element_type=jnp.float32)
        pieces = (
            lax.all_gather(real_low, "col", axis=1, tiled=True),
            lax.all_gather(imag_low, "col", axis=1, tiled=True),
        )
        strip = ham_columns
        right_real = jnp.dot(pieces[0], strip, preferred_element_type=jnp.float32)
        right_imag = jnp.dot(pieces[1], strip, preferred_element_type=jnp.float32)
        matrix = jnp.stack([real_part, imag_part])
        padded = extended(matrix.astype(jnp.bfloat16), (("row", 1), ("col", 2)), OMAX).astype(
            matrix.dtype
        )
        loss = dissipate(matrix, padded, amplitudes, offsets, active, row_first, col_first)
        return (left_imag - right_imag + loss[0], right_real - left_real + loss[1])

    first_real, first_imag = drift(rho_real, rho_imag)
    middle_real = rho_real + step_size * first_real
    middle_imag = rho_imag + step_size * first_imag
    rescale = levels / start_trace
    middle_real = middle_real * rescale
    middle_imag = middle_imag * rescale
    second_real, second_imag = drift(middle_real, middle_imag)
    updated_real = rho_real + 0.5 * step_size * (first_real + second_real)
    updated_imag = rho_imag + 0.5 * step_size * (first_imag + second_imag)
    rescale = levels / start_trace
    return (updated_real * rescale, updated_imag * rescale)


def solution(mesh):
    in_specs = (P("row", "col"), P("row", "col"), P("row", "col"), P(), P(), P())
    out_specs = (P("row", "col"), P("row", "col"))
    return jax.shard_map(local, mesh=mesh, in_specs=in_specs, out_specs=out_specs, check_vma=False)
```

profile of v0, /device:TPU:0, one launch (start us, length us, event | category | flops | bytes accessed | tf_op | source)
XLA Modules:
  0.0 739.0 jit_solution(2727342368948847065)
XLA Ops:
  7.2 2.7 convert_element_type.41
  15.4 4.9 collective-permute-start
  63.5 47.8 %psum.7 = f32[]{:T(128)} all-reduce(f32[]{:T(128)} %select_reduce_fusion), channel_id=1, replica_groups=mesh['row'=4,'col'=8] {'row','col'}, use_global_device_ids=true, to_apply=%region_1.2 | all-reduce | flops 1 | bytes 8 | tf_op jit(solution)/shard_map/psum | solution.py:67
  128.4 5.1 maximum_convert_fusion
  133.5 28.7 %select_add_fusion.1 = f32[2,1024,512]{2,1,0:T(8,128)} fusion(f32[2,1056,544]{2,1,0:T(8,128)} %maximum_convert_fusion, s32[]{:T(128)S(6)} %select_n.358, s32[]{:T(128)S(6)} %select_n.359, s32[]{:T(128)S(6)} %select_n.351, s32[]{:T(128)S(6)} %select_n.352, s32[]{:T(128)S(6)} %select_n.344, s32[]{:T(128)S(6)} %select_n.345, s32[]{:T(128)S(6)} %select_n.337, ...), kind=kLoop, calls=%fused_computation.3 | loop fusion | flops 41943040 | bytes 75497544 | tf_op jit(solution)/shard_map/add | solution.py:50
  162.2 10.7 %fusion.70 = f32[1024,512]{1,0:T(8,128)} fusion(bf16[1024,4096]{1,0:T(8,128)(2,1)} %all-gather.11.cloned.1.call-done, bf16[4096,512]{1,0:T(8,128)(2,1)} %all-gather.13.cloned.1.call-done), kind=kOutput, calls=%fused_computation.125 | convolution fusion | flops 4294967296 | bytes 14680064 | tf_op jit(solution)/shard_map/dot_general | solution.py:79
  172.9 61.1 %all-gather.17.cloned.1.call-done = bf16[4096,512]{1,0:T(8,128)(2,1)} async-done(((bf16[1024,512]{1,0:T(8,128)(2,1)}), bf16[4096,512]{1,0:T(8,128)(2,1)}) %all-gather.17.cloned.1.call-update) | async-done | bytes 4194320 | tf_op jit(solution)/shard_map/all_gather | solution.py:66
  234.0 56.1 %all-gather.15.cloned.1.call-done = bf16[1024,4096]{1,0:T(8,128)(2,1)} async-done(((bf16[1024,512]{1,0:T(8,128)(2,1)}), bf16[1024,4096]{1,0:T(8,128)(2,1)}) %all-gather.15.cloned.1.call-update) | async-done | bytes 8388624 | tf_op jit(solution)/shard_map/all_gather | solution.py:82
  290.2 10.5 %fusion.13 = f32[1024,512]{1,0:T(8,128)S(1)} fusion(f32[2,1024,512]{2,1,0:T(8,128)} %select_add_fusion.1, f32[1024,512]{1,0:T(8,128)} %fusion.70, bf16[1024,4096]{1,0:T(8,128)(2,1)} %all-gather.15.cloned.1.call-done, bf16[4096,512]{1,0:T(8,128)(2,1)} %all-gather.17.cloned.1.call-done), kind=kOutput, calls=%fused_computation.23 | convolution fusion | flops 4296015872 | bytes 18874368 | tf_op jit(solution)/shard_map/dot_general | solution.py:86
  305.7 53.7 %all-gather.19.cloned.1.call-done = bf16[1024,4096]{1,0:T(8,128)(2,1)} async-done(((bf16[1024,512]{1,0:T(8,128)(2,1)}), bf16[1024,4096]{1,0:T(8,128)(2,1)}) %all-gather.19.cloned.1.call-update) | async-done | bytes 8388624 | tf_op jit(solution)/shard_map/all_gather | solution.py:81
  359.4 10.5 %fusion.71 = f32[1024,512]{1,0:T(8,128)} fusion(bf16[1024,4096]{1,0:T(8,128)(2,1)} %all-gather.19.cloned.1.call-done, bf16[4096,512]{1,0:T(8,128)(2,1)} %all-gather.17.cloned.1.call-done), kind=kOutput, calls=%fused_computation.126 | convolution fusion | flops 4294967296 | bytes 14680064 | tf_op jit(solution)/shard_map/dot_general | solution.py:85
  369.8 71.7 %all-gather.21.cloned.1.call-done = bf16[4096,512]{1,0:T(8,128)(2,1)} async-done(((bf16[1024,512]{1,0:T(8,128)(2,1)}), bf16[4096,512]{1,0:T(8,128)(2,1)}) %all-gather.21.cloned.1.call-update) | async-done | bytes 4194320 | tf_op jit(solution)/shard_map/all_gather | solution.py:74
  441.6 10.3 %fusion.12 = f32[1024,512]{1,0:T(8,128)S(1)} fusion(f32[2,1024,512]{2,1,0:T(8,128)} %select_add_fusion.1, f32[1024,512]{1,0:T(8,128)} %fusion.71, bf16[1024,4096]{1,0:T(8,128)(2,1)} %all-gather.11.cloned.1.call-done, bf16[4096,512]{1,0:T(8,128)(2,1)} %all-gather.21.cloned.1.call-done), kind=kOutput, calls=%fused_computation.21 | convolution fusion | flops 4296015872 | bytes 18874368 | tf_op jit(solution)/shard_map/dot_general | solution.py:78
  461.3 4.3 collective-permute-done.5
  470.1 27.8 %all-gather.27.cloned.1.call-done = bf16[1024,4096]{1,0:T(8,128)(2,1)} async-done(((bf16[1024,512]{1,0:T(8,128)(2,1)}), bf16[1024,4096]{1,0:T(8,128)(2,1)}) %all-gather.27.cloned.1.call-update) | async-done | bytes 8388624 | tf_op jit(solution)/shard_map/all_gather | solution.py:81
  497.9 10.4 %fusion.73 = f32[1024,512]{1,0:T(8,128)} fusion(bf16[1024,4096]{1,0:T(8,128)(2,1)} %all-gather.27.cloned.1.call-done, bf16[4096,512]{1,0:T(8,128)(2,1)} %all-gather.17.cloned.1.call-done), kind=kOutput, calls=%fused_computation.128 | convolution fusion | flops 4294967296 | bytes 14680064 | tf_op jit(solution)/shard_map/dot_general | solution.py:85
  508.9 5.4 maximum_convert_fusion.1
  514.3 29.5 %select_add_fusion = f32[2,1024,512]{2,1,0:T(8,128)} fusion(f32[2,1056,544]{2,1,0:T(8,128)} %maximum_convert_fusion.1, s32[]{:T(128)S(6)} %select_n.358, s32[]{:T(128)S(6)} %select_n.359, s32[]{:T(128)S(6)} %select_n.351, s32[]{:T(128)S(6)} %select_n.352, s32[]{:T(128)S(6)} %select_n.344, s32[]{:T(128)S(6)} %select_n.345, s32[]{:T(128)S(6)} %select_n.337, ...), kind=kLoop, calls=%fused_computation.2 | loop fusion | flops 41943040 | bytes 75497544 | tf_op jit(solution)/shard_map/add | solution.py:50
  543.7 37.2 %all-gather.29.cloned.1.call-done = bf16[4096,512]{1,0:T(8,128)(2,1)} async-done(((bf16[1024,512]{1,0:T(8,128)(2,1)}), bf16[4096,512]{1,0:T(8,128)(2,1)}) %all-gather.29.cloned.1.call-update) | async-done | bytes 4194320 | tf_op jit(solution)/shard_map/all_gather | solution.py:74
  580.9 12.5 %fusion.6 = f32[1024,512]{1,0:T(8,128)} fusion(f32[1024,512]{1,0:T(8,128)S(1)} %copy-done, f32[1024,512]{1,0:T(8,128)} %copy-done.8, f32[2,1024,512]{2,1,0:T(8,128)} %select_add_fusion, f32[1024,512]{1,0:T(8,128)} %fusion.73, bf16[1024,4096]{1,0:T(8,128)(2,1)} %all-gather.11.cloned.1.call-done, bf16[4096,512]{1,0:T(8,128)(2,1)} %all-gather.29.cloned.1.call-done, ...), kind=kOutput, calls=%fused_computation.13 | convolution fusion | flops 4298113024 | bytes 23068676 | tf_op jit(solution)/shard_map/dot_general | solution.py:78
  593.4 43.8 %all-gather.25.cloned.1.call-done = bf16[1024,4096]{1,0:T(8,128)(2,1)} async-done(((bf16[1024,512]{1,0:T(8,128)(2,1)}), bf16[1024,4096]{1,0:T(8,128)(2,1)}) %all-gather.25.cloned.1.call-update) | async-done | bytes 8388624 | tf_op jit(solution)/shard_map/all_gather | solution.py:82
  637.2 10.5 %fusion.72 = f32[1024,512]{1,0:T(8,128)} fusion(bf16[1024,4096]{1,0:T(8,128)(2,1)} %all-gather.25.cloned.1.call-done, bf16[4096,512]{1,0:T(8,128)(2,1)} %all-gather.17.cloned.1.call-done), kind=kOutput, calls=%fused_computation.127 | convolution fusion | flops 4294967296 | bytes 14680064 | tf_op jit(solution)/shard_map/dot_general | solution.py:86
  647.7 71.7 %all-gather.23.cloned.1.call-done = bf16[4096,512]{1,0:T(8,128)(2,1)} async-done(((bf16[1024,512]{1,0:T(8,128)(2,1)}), bf16[4096,512]{1,0:T(8,128)(2,1)}) %all-gather.23.cloned.1.call-update) | async-done | bytes 4194320 | tf_op jit(solution)/shard_map/all_gather | solution.py:75
  719.4 12.5 %fusion.11 = f32[1024,512]{1,0:T(8,128)} fusion(f32[1024,512]{1,0:T(8,128)S(1)} %copy-done.3, f32[1024,512]{1,0:T(8,128)} %copy-done.7, f32[2,1024,512]{2,1,0:T(8,128)} %select_add_fusion, f32[1024,512]{1,0:T(8,128)} %fusion.72, bf16[1024,4096]{1,0:T(8,128)(2,1)} %all-gather.11.cloned.1.call-done, bf16[4096,512]{1,0:T(8,128)(2,1)} %all-gather.23.cloned.1.call-done, ...), kind=kOutput, calls=%fused_computation.19 | convolution fusion | flops 4298113024 | bytes 23068676 | tf_op jit(solution)/shard_map/dot_general | solution.py:79
  (127 shorter events, 58.2 us)
Async XLA Ops:
  7.2 155.0 %all-gather.13.cloned.1.call-start = ((), (), s32[]{:S(2)}) async-start(), calls=%async_computation.1 | async-start | bytes 5242880 | tf_op jit(solution)/shard_map/all_gather | solution.py:75
  10.0 152.2 %all-gather.11.cloned.1.call-start = ((), (), s32[]{:S(2)}) async-start(), calls=%async_computation | async-start | bytes 9437184 | tf_op jit(solution)/shard_map/all_gather | solution.py:72
  10.7 223.3 %all-gather.17.cloned.1.call-start = ((), (), s32[]{:S(2)}) async-start(), calls=%async_computation.3 | async-start | bytes 5242880 | tf_op jit(solution)/shard_map/all_gather | solution.py:66
  11.4 278.7 %all-gather.15.cloned.1.call-start = ((), (), s32[]{:S(2)}) async-start(), calls=%async_computation.2 | async-start | bytes 9437184 | tf_op jit(solution)/shard_map/all_gather | solution.py:82
  12.0 347.3 %all-gather.19.cloned.1.call-start = ((), (), s32[]{:S(2)}) async-start(), calls=%async_computation.4 | async-start | bytes 9437184 | tf_op jit(solution)/shard_map/all_gather | solution.py:81
  12.1 9.6 %copy-start.10 = (s32[8]{0:T(128)S(1)}, s32[8]{0:T(128)}, u32[]{:S(2)}) copy-start(s32[8]{0:T(128)} %param.10) | copy-start | bytes 100
  12.1 20.4 %copy-start.9 = (f32[8,4096]{1,0:T(8,128)S(1)}, f32[8,4096]{1,0:T(8,128)}, u32[]{:S(2)}) copy-start(f32[8,4096]{1,0:T(8,128)} %param.9) | copy-start | bytes 393220
  15.4 42.2 %collective-permute-start = (bf16[2,16,512]{2,1,0:T(8,128)(2,1)S(1)}, bf16[2,16,512]{2,1,0:T(8,128)(2,1)S(1)}, u32[]{:S(2)}, u32[]{:S(2)}) collective-permute-start(bf16[2,16,512]{2,1,0:T(8,128)(2,1)S(1)} %get-tuple-element.29), channel_id=1, source_target_pairs={{0,8},{8,16},{16,24},{1,9},{9,17},{17,25},{2,10},{10,18},{18,26},{... | collective-permute-start | bytes 98312 | tf_op jit(solution)/shard_map/ppermute | solution.py:18
  20.4 37.3 %collective-permute-start.1 = (bf16[2,16,512]{2,1,0:T(8,128)(2,1)S(1)}, bf16[2,16,512]{2,1,0:T(8,128)(2,1)S(1)}, u32[]{:S(2)}, u32[]{:S(2)}) collective-permute-start(bf16[2,16,512]{2,1,0:T(8,128)(2,1)S(1)} %get-tuple-element.30), channel_id=1, source_target_pairs={{8,0},{16,8},{24,16},{9,1},{17,9},{25,17},{10,2},{18,10},{26,18},{... | collective-permute-start | bytes 98312 | tf_op jit(solution)/shard_map/ppermute | solution.py:20
  53.7 3.9 copy-start.5
  58.1 69.7 %collective-permute-start.2 = (bf16[2,1056,16]{1,2,0:T(8,128)(2,1)S(1)}, bf16[2,1056,16]{1,2,0:T(8,128)(2,1)S(1)}, u32[]{:S(2)}, u32[]{:S(2)}) collective-permute-start(bf16[2,1056,16]{1,2,0:T(8,128)(2,1)S(1)} %copy.10), channel_id=1, source_target_pairs={{0,1},{1,2},{2,3},{3,4},{4,5},{5,6},{6,7},{8,9},{9,10},{10,11},{11... | collective-permute-start | bytes 202760 | tf_op jit(solution)/shard_map/ppermute | solution.py:18
  59.8 68.3 %collective-permute-start.3 = (bf16[2,1056,16]{1,2,0:T(8,128)(2,1)S(1)}, bf16[2,1056,16]{1,2,0:T(8,128)(2,1)S(1)}, u32[]{:S(2)}, u32[]{:S(2)}) collective-permute-start(bf16[2,1056,16]{1,2,0:T(8,128)(2,1)S(1)} %copy.11), channel_id=1, source_target_pairs={{1,0},{2,1},{3,2},{4,3},{5,4},{6,5},{7,6},{9,8},{10,9},{11,10},{12... | collective-permute-start | bytes 202760 | tf_op jit(solution)/shard_map/ppermute | solution.py:20
  290.1 10.5 %copy-start.2 = (f32[1024,512]{1,0:T(8,128)S(1)}, f32[1024,512]{1,0:T(8,128)}, u32[]{:S(2)}) copy-start(f32[1024,512]{1,0:T(8,128)} %param.6) | copy-start | bytes 6291460
  300.6 2.7 copy-start.7
  303.4 138.2 %all-gather.21.cloned.1.call-start = ((), (), s32[]{:S(2)}) async-start(), calls=%async_computation.5 | async-start | bytes 5242880 | tf_op jit(solution)/shard_map/all_gather | solution.py:74
  303.9 194.0 %all-gather.27.cloned.1.call-start = ((), (), s32[]{:S(2)}) async-start(), calls=%async_computation.8 | async-start | bytes 9437184 | tf_op jit(solution)/shard_map/all_gather | solution.py:81
  304.7 276.3 %all-gather.29.cloned.1.call-start = ((), (), s32[]{:S(2)}) async-start(), calls=%async_computation.9 | async-start | bytes 5242880 | tf_op jit(solution)/shard_map/all_gather | solution.py:74
  305.4 331.8 %all-gather.25.cloned.1.call-start = ((), (), s32[]{:S(2)}) async-start(), calls=%async_computation.7 | async-start | bytes 9437184 | tf_op jit(solution)/shard_map/all_gather | solution.py:82
  454.4 265.0 %all-gather.23.cloned.1.call-start = ((), (), s32[]{:S(2)}) async-start(), calls=%async_computation.6 | async-start | bytes 5242880 | tf_op jit(solution)/shard_map/all_gather | solution.py:75
  458.4 2.9 collective-permute-start.4
  459.7 5.9 collective-permute-start.5
  467.3 41.0 %collective-permute-start.6 = (bf16[2,1056,16]{1,2,0:T(8,128)(2,1)S(1)}, bf16[2,1056,16]{1,2,0:T(8,128)(2,1)S(1)}, u32[]{:S(2)}, u32[]{:S(2)}) collective-permute-start(bf16[2,1056,16]{1,2,0:T(8,128)(2,1)S(1)} %copy.15), channel_id=1, source_target_pairs={{0,1},{1,2},{2,3},{3,4},{4,5},{5,6},{6,7},{8,9},{9,10},{10,11},{11... | collective-permute-start | bytes 202760 | tf_op jit(solution)/shard_map/ppermute | solution.py:18
  468.8 39.8 %collective-permute-start.7 = (bf16[2,1056,16]{1,2,0:T(8,128)(2,1)S(1)}, bf16[2,1056,16]{1,2,0:T(8,128)(2,1)S(1)}, u32[]{:S(2)}, u32[]{:S(2)}) collective-permute-start(bf16[2,1056,16]{1,2,0:T(8,128)(2,1)S(1)} %copy.16), channel_id=1, source_target_pairs={{1,0},{2,1},{3,2},{4,3},{5,4},{6,5},{7,6},{9,8},{10,9},{11,10},{12... | collective-permute-start | bytes 202760 | tf_op jit(solution)/shard_map/ppermute | solution.py:20
  593.4 126.0 %copy-start.3 = (f32[1024,512]{1,0:T(8,128)S(1)}, f32[1024,512]{1,0:T(8,128)}, u32[]{:S(2)}) copy-start(f32[1024,512]{1,0:T(8,128)} %param.6) | copy-start | bytes 6291460
  (5 other events, 9.8 us)
Sparse Core Ops, SparseCore 0:
  10.1 84.7 all-gather.12
  96.7 54.9 all-gather.10
  153.3 80.7 all-gather.16
  235.8 54.3 all-gather.14
  303.5 55.8 all-gather.18
  360.8 80.7 all-gather.20
  443.4 54.4 all-gather.26
  499.5 81.4 all-gather.28
  582.8 54.3 all-gather.24
  638.6 80.7 all-gather.22
where the time goes:
time: 744 us; the launch traced here: 739 us
  waiting for transfers between devices  432 us (58%)
  other arithmetic  108 us (15%)
  matrix products  87.7 us (12%)
  blocking collectives  47.8 us (6%)
  between operations  41.4 us (6%)
  starting transfers between devices  14.7 us (2%)
    all_gather x2, waiting for transfers between devices, drift(): lax.all_gather(real_low, 'row', axis=0, tiled=True)  109 us
    all_gather x2, waiting for transfers between devices, drift(): lax.all_gather(imag_low, 'col', axis=1, tiled=True)  99.9 us
    all_gather x2, waiting for transfers between devices, drift(): lax.all_gather(real_low, 'col', axis=1, tiled=True)  81.5 us
    all_gather x2, waiting for transfers between devices, drift(): lax.all_gather(imag_low, 'row', axis=0, tiled=True)  71.7 us
    all_gather x1, waiting for transfers between devices, local(): ham_columns = lax.all_gather(hamiltonian, 'row', axis=0, tiled=True)  61.1 us
    add x2, other arithmetic, dissipate(): summed = summed + jnp.where(jump_slot < active, contribution, 0.0)  58.1 us
    psum x1, blocking collectives, local(): lax.psum(diagonal_sum(rho_real, row_first, col_first), ('row', 'col'))  47.8 us
    dot_general x2, matrix products, drift(): left_imag = jnp.dot(strip, pieces[1], preferred_element_type=jnp.float32)  23.2 us
  transfers between devices with their start and end apart: 18, of which 10 were waited for; matrix products, arithmetic and copies ran while one was open for 23% of the time, Pallas kernels for 0%

commit v1 on v0

--- a/solution.py
+++ b/solution.py
@@ -5,6 +5,17 @@
 
 OMAX = 16
 step_size = 0.25
+
+
+def pass_along(value, axis, dim):
+    peers = lax.axis_size(axis)
+    forward = [(i, (i + 1) % peers) for i in range(peers)]
+    parts = [value]
+    for stride in range(1, peers):
+        parts = [lax.ppermute(parts[0], axis, forward), *parts]
+    whole = jnp.concatenate(parts, axis=dim)
+    shift = (lax.axis_index(axis) + 1) * parts[-1].shape[dim]
+    return jnp.roll(whole, shift, axis=dim)
 
 
 def extended(cells, sides, width):
@@ -63,7 +74,7 @@
     row_first = lax.axis_index("row") * height
     col_first = lax.axis_index("col") * breadth
     active = active_jumps[0]
-    ham_columns = lax.all_gather(hamiltonian, "row", axis=0, tiled=True)
+    ham_columns = pass_along(hamiltonian, "row", 0)
     start_trace = lax.psum(diagonal_sum(rho_real, row_first, col_first), ("row", "col"))
 
     def drift(real_part, imag_part):

time: 744 us -> 701 us (0.942)
  waiting for transfers between devices: 432 us -> 326 us
  blocking collectives: 47.8 us -> 70.9 us
  local copies, waits for them, and re-layouts: 7.37 us -> 27 us
  starting transfers between devices: 14.7 us -> 33.5 us
    all_gather x1 -> x0, waiting for transfers between devices: 61.1 us -> none  [local(): ham_columns = lax.all_gather(hamiltonian, 'row', axis=0, tiled=True)]
    all_gather x2, waiting for transfers between devices: 99.9 us -> 60.6 us  [drift(): lax.all_gather(imag_low, 'col', axis=1, tiled=True)]
    all_gather x2, waiting for transfers between devices: 81.5 us -> 55.8 us  [drift(): lax.all_gather(real_low, 'col', axis=1, tiled=True)]
    psum x1, blocking collectives: 47.8 us -> 70.9 us  [local(): lax.psum(diagonal_sum(rho_real, row_first, col_first), ('row', 'col'))]
    all_gather x2, waiting for transfers between devices: 109 us -> 130 us  [drift(): lax.all_gather(real_low, 'row', axis=0, tiled=True)]
    ppermute x0 -> x3, starting transfers between devices: none -> 17.7 us  [pass_along(): parts = [lax.ppermute(parts[0], axis, forward), *parts]]
    unnamed x22 -> x31, local copies, waits for them, and re-layouts: 2.66 us -> 17.7 us
  transfers between devices with their start and end apart: 18 -> 20, of which waited for: 10 -> 9; matrix products, arithmetic and copies ran while one was open for 23% -> 28% of each run, Pallas kernels for 0% -> 0%
where the time goes in v1:
time: 701 us; the launch traced here: 693 us
  waiting for transfers between devices  326 us (47%)
  other arithmetic  108 us (15%)
  matrix products  87.7 us (13%)
  blocking collectives  70.9 us (10%)
  between operations  40.1 us (6%)
  starting transfers between devices  33.5 us (5%)
  local copies, waits for them, and re-layouts  27 us (4%)
    all_gather x2, waiting for transfers between devices, drift(): lax.all_gather(real_low, 'row', axis=0, tiled=True)  130 us
    psum x1, blocking collectives, local(): lax.psum(diagonal_sum(rho_real, row_first, col_first), ('row', 'col'))  70.9 us
    all_gather x2, waiting for transfers between devices, drift(): lax.all_gather(imag_low, 'row', axis=0, tiled=True)  69.9 us
    all_gather x2, waiting for transfers between devices, drift(): lax.all_gather(imag_low, 'col', axis=1, tiled=True)  60.6 us
    add x2, other arithmetic, dissipate(): summed = summed + jnp.where(jump_slot < active, contribution, 0.0)  59 us
    all_gather x2, waiting for transfers between devices, drift(): lax.all_gather(real_low, 'col', axis=1, tiled=True)  55.8 us
    dot_general x2, matrix products, drift(): right_imag = jnp.dot(pieces[1], strip, preferred_element_type=jnp.float32)  22.9 us
    dot_general x2, matrix products, drift(): right_real = jnp.dot(pieces[0], strip, preferred_element_type=jnp.float32)  22.8 us
  transfers between devices with their start and end apart: 20, of which 9 were waited for; matrix products, arithmetic and copies ran while one was open for 28% of the time, Pallas kernels for 0%

profile of v1, /device:TPU:0, one launch (start us, length us, event | category | flops | bytes accessed | tf_op | source)
XLA Modules:
  0.0 693.2 jit_solution(11660752191076876711)
XLA Ops:
  18.1 3.5 collective-permute-start.3
  58.1 14.2 %collective-permute-start.1 = (bf16[1024,512]{1,0:T(8,128)(2,1)}, bf16[1024,512]{1,0:T(8,128)(2,1)}, u32[]{:S(2)}, u32[]{:S(2)}) collective-permute-start(bf16[1024,512]{1,0:T(8,128)(2,1)} %collective-permute-done), channel_id=1, source_target_pairs={{0,8},{8,16},{16,24},{24,0},{1,9},{9,17},{17,25},{25,1},{2,10},{10... | collective-permute-start | bytes 3145736 | tf_op jit(solution)/shard_map/ppermute | solution.py:15
  80.9 70.9 %psum.7 = f32[]{:T(128)} all-reduce(f32[]{:T(128)} %select_reduce_fusion), channel_id=1, replica_groups=mesh['row'=4,'col'=8] {'row','col'}, use_global_device_ids=true, to_apply=%region_1.2 | all-reduce | flops 1 | bytes 8 | tf_op jit(solution)/shard_map/psum | solution.py:78
  169.7 5.2 maximum_convert_fusion
  175.4 29.2 %select_add_fusion.1 = f32[2,1024,512]{2,1,0:T(8,128)} fusion(f32[2,1056,544]{2,1,0:T(8,128)} %maximum_convert_fusion, s32[]{:T(128)S(6)} %select_n.373, s32[]{:T(128)S(6)} %select_n.374, s32[]{:T(128)S(6)} %select_n.366, s32[]{:T(128)S(6)} %select_n.367, s32[]{:T(128)S(6)} %select_n.359, s32[]{:T(128)S(6)} %select_n.360, s32[]{:T(128)S(6)} %select_n.352, ...), kind=kLoop, calls=%fused_computation.3 | loop fusion | flops 41943040 | bytes 75497544 | tf_op jit(solution)/shard_map/add | solution.py:61
  220.7 10.6 %fusion.90 = f32[1024,512]{1,0:T(8,128)} fusion(bf16[1024,4096]{1,0:T(8,128)(2,1)} %all-gather.10.cloned.1.call-done, bf16[4096,512]{1,0:T(8,128)(2,1)} %all-gather.12.cloned.1.call-done), kind=kOutput, calls=%fused_computation.147 | convolution fusion | flops 4294967296 | bytes 14680064 | tf_op jit(solution)/shard_map/dot_general | solution.py:90
  231.3 14.7 %all-gather.14.cloned.1.call-done = bf16[1024,4096]{1,0:T(8,128)(2,1)} async-done(((bf16[1024,512]{1,0:T(8,128)(2,1)}), bf16[1024,4096]{1,0:T(8,128)(2,1)}) %all-gather.14.cloned.1.call-update) | async-done | bytes 8388624 | tf_op jit(solution)/shard_map/all_gather | solution.py:93
  246.0 10.5 %fusion.21 = f32[1024,512]{1,0:T(8,128)S(1)} fusion(f32[2,1024,512]{2,1,0:T(8,128)} %select_add_fusion.1, f32[1024,512]{1,0:T(8,128)} %fusion.90, bf16[1024,4096]{1,0:T(8,128)(2,1)} %all-gather.14.cloned.1.call-done, bf16[8192,512]{1,0:T(8,128)(2,1)} %constant_dynamic-update-slice_fusion, s32[]{:T(128)S(6)} %select_n.317), kind=kOutput, calls=%fused_computation.31 | convolution fusion | flops 4296015872 | bytes 18874372 | tf_op jit(solution)/shard_map/dot_general | solution.py:97
  261.4 78.8 %all-gather.18.cloned.1.call-done = bf16[4096,512]{1,0:T(8,128)(2,1)} async-done(((bf16[1024,512]{1,0:T(8,128)(2,1)}), bf16[4096,512]{1,0:T(8,128)(2,1)}) %all-gather.18.cloned.1.call-update) | async-done | bytes 4194320 | tf_op jit(solution)/shard_map/all_gather | solution.py:85
  340.1 10.3 %fusion.91 = f32[1024,512]{1,0:T(8,128)} fusion(bf16[1024,4096]{1,0:T(8,128)(2,1)} %all-gather.10.cloned.1.call-done, bf16[4096,512]{1,0:T(8,128)(2,1)} %all-gather.18.cloned.1.call-done), kind=kOutput, calls=%fused_computation.148 | convolution fusion | flops 4294967296 | bytes 14680064 | tf_op jit(solution)/shard_map/dot_general | solution.py:89
  350.5 45.8 %all-gather.16.cloned.1.call-done = bf16[1024,4096]{1,0:T(8,128)(2,1)} async-done(((bf16[1024,512]{1,0:T(8,128)(2,1)}), bf16[1024,4096]{1,0:T(8,128)(2,1)}) %all-gather.16.cloned.1.call-update) | async-done | bytes 8388624 | tf_op jit(solution)/shard_map/all_gather | solution.py:92
  396.2 10.3 %fusion.20 = f32[1024,512]{1,0:T(8,128)S(1)} fusion(f32[2,1024,512]{2,1,0:T(8,128)} %select_add_fusion.1, f32[1024,512]{1,0:T(8,128)} %fusion.91, bf16[1024,4096]{1,0:T(8,128)(2,1)} %all-gather.16.cloned.1.call-done, bf16[8192,512]{1,0:T(8,128)(2,1)} %constant_dynamic-update-slice_fusion, s32[]{:T(128)S(6)} %select_n.317), kind=kOutput, calls=%fused_computation.29 | convolution fusion | flops 4296015872 | bytes 18874372 | tf_op jit(solution)/shard_map/dot_general | solution.py:96
  413.4 3.4 collective-permute-start.7
  419.1 4.6 collective-permute-done.8
  427.6 51.5 %all-gather.26.cloned.1.call-done = bf16[4096,512]{1,0:T(8,128)(2,1)} async-done(((bf16[1024,512]{1,0:T(8,128)(2,1)}), bf16[4096,512]{1,0:T(8,128)(2,1)}) %all-gather.26.cloned.1.call-update) | async-done | bytes 4194320 | tf_op jit(solution)/shard_map/all_gather | solution.py:85
  479.1 10.6 %fusion.93 = f32[512,1024]{0,1:T(8,128)} fusion(bf16[1024,4096]{1,0:T(8,128)(2,1)} %all-gather.10.cloned.1.call-done, bf16[4096,512]{1,0:T(8,128)(2,1)} %all-gather.26.cloned.1.call-done), kind=kOutput, calls=%fused_computation.150 | convolution fusion | flops 4294967296 | bytes 14680064 | tf_op jit(solution)/shard_map/dot_general | solution.py:89
  490.3 5.3 maximum_convert_fusion.1
  495.6 29.7 %select_add_fusion = f32[2,1024,512]{2,1,0:T(8,128)} fusion(f32[2,1056,544]{2,1,0:T(8,128)} %maximum_convert_fusion.1, s32[]{:T(128)S(6)} %select_n.373, s32[]{:T(128)S(6)} %select_n.374, s32[]{:T(128)S(6)} %select_n.366, s32[]{:T(128)S(6)} %select_n.367, s32[]{:T(128)S(6)} %select_n.359, s32[]{:T(128)S(6)} %select_n.360, s32[]{:T(128)S(6)} %select_n.352, ...), kind=kLoop, calls=%fused_computation.2 | loop fusion | flops 41943040 | bytes 75497544 | tf_op jit(solution)/shard_map/add | solution.py:61
  525.3 10.1 %all-gather.24.cloned.1.call-done = bf16[1024,4096]{1,0:T(8,128)(2,1)} async-done(((bf16[1024,512]{1,0:T(8,128)(2,1)}), bf16[1024,4096]{1,0:T(8,128)(2,1)}) %all-gather.24.cloned.1.call-update) | async-done | bytes 8388624 | tf_op jit(solution)/shard_map/all_gather | solution.py:92
  535.4 12.5 %fusion.14 = f32[1024,512]{1,0:T(8,128)} fusion(f32[1024,512]{1,0:T(8,128)S(1)} %copy-done, f32[1024,512]{1,0:T(8,128)} %copy-done.9, f32[2,1024,512]{2,1,0:T(8,128)} %select_add_fusion, f32[512,1024]{0,1:T(8,128)} %fusion.93, bf16[1024,4096]{1,0:T(8,128)(2,1)} %all-gather.24.cloned.1.call-done, bf16[8192,512]{1,0:T(8,128)(2,1)} %constant_dynamic-update-slice_fusion, ...), kind=kOutput, calls=%fused_computation.21 | convolution fusion | flops 4298113024 | bytes 23068680 | tf_op jit(solution)/shard_map/dot_general | solution.py:96
  547.8 69.9 %all-gather.20.cloned.1.call-done = bf16[4096,512]{1,0:T(8,128)(2,1)} async-done(((bf16[1024,512]{1,0:T(8,128)(2,1)}), bf16[4096,512]{1,0:T(8,128)(2,1)}) %all-gather.20.cloned.1.call-update) | async-done | bytes 4194320 | tf_op jit(solution)/shard_map/all_gather | solution.py:86
  617.7 10.4 %fusion.92 = f32[512,1024]{0,1:T(8,128)} fusion(bf16[1024,4096]{1,0:T(8,128)(2,1)} %all-gather.10.cloned.1.call-done, bf16[4096,512]{1,0:T(8,128)(2,1)} %all-gather.20.cloned.1.call-done), kind=kOutput, calls=%fused_computation.149 | convolution fusion | flops 4294967296 | bytes 14680064 | tf_op jit(solution)/shard_map/dot_general | solution.py:90
  628.1 45.9 %all-gather.22.cloned.1.call-done = bf16[1024,4096]{1,0:T(8,128)(2,1)} async-done(((bf16[1024,512]{1,0:T(8,128)(2,1)}), bf16[1024,4096]{1,0:T(8,128)(2,1)}) %all-gather.22.cloned.1.call-update) | async-done | bytes 8388624 | tf_op jit(solution)/shard_map/all_gather | solution.py:93
  674.0 12.5 %fusion.19 = f32[1024,512]{1,0:T(8,128)} fusion(f32[1024,512]{1,0:T(8,128)S(1)} %copy-done.3, f32[1024,512]{1,0:T(8,128)} %copy-done.8, f32[2,1024,512]{2,1,0:T(8,128)} %select_add_fusion, f32[512,1024]{0,1:T(8,128)} %fusion.92, bf16[1024,4096]{1,0:T(8,128)(2,1)} %all-gather.22.cloned.1.call-done, bf16[8192,512]{1,0:T(8,128)(2,1)} %constant_dynamic-update-slice_fusion, ...), kind=kOutput, calls=%fused_computation.27 | convolution fusion | flops 4298113024 | bytes 23068680 | tf_op jit(solution)/shard_map/dot_general | solution.py:97
  (140 shorter events, 82.9 us)
Async XLA Ops:
  7.2 213.5 %all-gather.12.cloned.1.call-start = ((), (), s32[]{:S(2)}) async-start(), calls=%async_computation.1 | async-start | bytes 5242880 | tf_op jit(solution)/shard_map/all_gather | solution.py:86
  10.2 12.7 %copy-start.11 = (s32[8]{0:T(128)S(1)}, s32[8]{0:T(128)}, u32[]{:S(2)}) copy-start(s32[8]{0:T(128)} %param.10) | copy-start | bytes 100
  10.2 23.2 %copy-start.10 = (f32[8,4096]{1,0:T(8,128)S(1)}, f32[8,4096]{1,0:T(8,128)}, u32[]{:S(2)}) copy-start(f32[8,4096]{1,0:T(8,128)} %param.9) | copy-start | bytes 393220
  10.2 210.5 %all-gather.10.cloned.1.call-start = ((), (), s32[]{:S(2)}) async-start(), calls=%async_computation | async-start | bytes 9437184 | tf_op jit(solution)/shard_map/all_gather | solution.py:83
  10.9 235.0 %all-gather.14.cloned.1.call-start = ((), (), s32[]{:S(2)}) async-start(), calls=%async_computation.2 | async-start | bytes 9437184 | tf_op jit(solution)/shard_map/all_gather | solution.py:93
  11.7 328.5 %all-gather.18.cloned.1.call-start = ((), (), s32[]{:S(2)}) async-start(), calls=%async_computation.4 | async-start | bytes 5242880 | tf_op jit(solution)/shard_map/all_gather | solution.py:85
  11.7 46.3 %collective-permute-start = (bf16[1024,512]{1,0:T(8,128)(2,1)S(1)}, bf16[1024,512]{1,0:T(8,128)(2,1)}, u32[]{:S(2)}, u32[]{:S(2)}) collective-permute-start(bf16[1024,512]{1,0:T(8,128)(2,1)S(1)} %copy-done.7), channel_id=1, source_target_pairs={{0,8},{8,16},{16,24},{24,0},{1,9},{9,17},{17,25},{25,1},{2,10},{10... | collective-permute-start | bytes 3145736 | tf_op jit(solution)/shard_map/ppermute | solution.py:15
  18.1 54.1 %collective-permute-start.3 = (bf16[2,16,512]{2,1,0:T(8,128)(2,1)S(1)}, bf16[2,16,512]{2,1,0:T(8,128)(2,1)S(1)}, u32[]{:S(2)}, u32[]{:S(2)}) collective-permute-start(bf16[2,16,512]{2,1,0:T(8,128)(2,1)S(1)} %get-tuple-element.29), channel_id=1, source_target_pairs={{0,8},{8,16},{16,24},{1,9},{9,17},{17,25},{2,10},{10,18},{18,26},{... | collective-permute-start | bytes 98312 | tf_op jit(solution)/shard_map/ppermute | solution.py:29
  21.6 50.6 %collective-permute-start.4 = (bf16[2,16,512]{2,1,0:T(8,128)(2,1)S(1)}, bf16[2,16,512]{2,1,0:T(8,128)(2,1)S(1)}, u32[]{:S(2)}, u32[]{:S(2)}) collective-permute-start(bf16[2,16,512]{2,1,0:T(8,128)(2,1)S(1)} %get-tuple-element.30), channel_id=1, source_target_pairs={{8,0},{16,8},{24,16},{9,1},{17,9},{25,17},{10,2},{18,10},{26,18},{... | collective-permute-start | bytes 98312 | tf_op jit(solution)/shard_map/ppermute | solution.py:31
  54.3 17.9 %copy-start.5 = (bf16[2,1024,512]{2,1,0:T(8,128)(2,1)S(1)}, bf16[2,1024,512]{2,1,0:T(8,128)(2,1)}, u32[]{:S(2)}) copy-start(bf16[2,1024,512]{2,1,0:T(8,128)(2,1)} %copy-done.4) | copy-start | bytes 6291460
  58.1 116.8 %collective-permute-start.1 = (bf16[1024,512]{1,0:T(8,128)(2,1)}, bf16[1024,512]{1,0:T(8,128)(2,1)}, u32[]{:S(2)}, u32[]{:S(2)}) collective-permute-start(bf16[1024,512]{1,0:T(8,128)(2,1)} %collective-permute-done), channel_id=1, source_target_pairs={{0,8},{8,16},{16,24},{24,0},{1,9},{9,17},{17,25},{25,1},{2,10},{10... | collective-permute-start | bytes 3145736 | tf_op jit(solution)/shard_map/ppermute | solution.py:15
  74.7 92.9 %collective-permute-start.5 = (bf16[2,1056,16]{1,2,0:T(8,128)(2,1)S(1)}, bf16[2,1056,16]{1,2,0:T(8,128)(2,1)S(1)}, u32[]{:S(2)}, u32[]{:S(2)}) collective-permute-start(bf16[2,1056,16]{1,2,0:T(8,128)(2,1)S(1)} %copy.13), channel_id=1, source_target_pairs={{0,1},{1,2},{2,3},{3,4},{4,5},{5,6},{6,7},{8,9},{9,10},{10,11},{11... | collective-permute-start | bytes 202760 | tf_op jit(solution)/shard_map/ppermute | solution.py:29
  77.3 91.4 %collective-permute-start.6 = (bf16[2,1056,16]{1,2,0:T(8,128)(2,1)S(1)}, bf16[2,1056,16]{1,2,0:T(8,128)(2,1)S(1)}, u32[]{:S(2)}, u32[]{:S(2)}) collective-permute-start(bf16[2,1056,16]{1,2,0:T(8,128)(2,1)S(1)} %copy.14), channel_id=1, source_target_pairs={{1,0},{2,1},{3,2},{4,3},{5,4},{6,5},{7,6},{9,8},{10,9},{11,10},{12... | collective-permute-start | bytes 202760 | tf_op jit(solution)/shard_map/ppermute | solution.py:31
  174.9 29.7 %collective-permute-start.2 = (bf16[1024,512]{1,0:T(8,128)(2,1)}, bf16[1024,512]{1,0:T(8,128)(2,1)}, u32[]{:S(2)}, u32[]{:S(2)}) collective-permute-start(bf16[1024,512]{1,0:T(8,128)(2,1)} %collective-permute-done.1), channel_id=1, source_target_pairs={{0,8},{8,16},{16,24},{24,0},{1,9},{9,17},{17,25},{25,1},{2,10},{10... | collective-permute-start | bytes 3145736 | tf_op jit(solution)/shard_map/ppermute | solution.py:15
  259.2 137.0 %all-gather.16.cloned.1.call-start = ((), (), s32[]{:S(2)}) async-start(), calls=%async_computation.3 | async-start | bytes 9437184 | tf_op jit(solution)/shard_map/all_gather | solution.py:92
  259.8 219.3 %all-gather.26.cloned.1.call-start = ((), (), s32[]{:S(2)}) async-start(), calls=%async_computation.8 | async-start | bytes 5242880 | tf_op jit(solution)/shard_map/all_gather | solution.py:85
  260.4 274.9 %all-gather.24.cloned.1.call-start = ((), (), s32[]{:S(2)}) async-start(), calls=%async_computation.7 | async-start | bytes 9437184 | tf_op jit(solution)/shard_map/all_gather | solution.py:92
  261.2 356.5 %all-gather.20.cloned.1.call-start = ((), (), s32[]{:S(2)}) async-start(), calls=%async_computation.5 | async-start | bytes 5242880 | tf_op jit(solution)/shard_map/all_gather | solution.py:86
  410.1 263.9 %all-gather.22.cloned.1.call-start = ((), (), s32[]{:S(2)}) async-start(), calls=%async_computation.6 | async-start | bytes 9437184 | tf_op jit(solution)/shard_map/all_gather | solution.py:93
  413.4 5.7 collective-permute-start.7
  416.8 6.9 collective-permute-start.8
  424.2 65.5 %collective-permute-start.9 = (bf16[2,1056,16]{1,2,0:T(8,128)(2,1)S(1)}, bf16[2,1056,16]{1,2,0:T(8,128)(2,1)S(1)}, u32[]{:S(2)}, u32[]{:S(2)}) collective-permute-start(bf16[2,1056,16]{1,2,0:T(8,128)(2,1)S(1)} %copy.19), channel_id=1, source_target_pairs={{0,1},{1,2},{2,3},{3,4},{4,5},{5,6},{6,7},{8,9},{9,10},{10,11},{11... | collective-permute-start | bytes 202760 | tf_op jit(solution)/shard_map/ppermute | solution.py:29
  426.3 63.7 %collective-permute-start.10 = (bf16[2,1056,16]{1,2,0:T(8,128)(2,1)S(1)}, bf16[2,1056,16]{1,2,0:T(8,128)(2,1)S(1)}, u32[]{:S(2)}, u32[]{:S(2)}) collective-permute-start(bf16[2,1056,16]{1,2,0:T(8,128)(2,1)S(1)} %copy.20), channel_id=1, source_target_pairs={{1,0},{2,1},{3,2},{4,3},{5,4},{6,5},{7,6},{9,8},{10,9},{11,10},{12... | collective-permute-start | bytes 202760 | tf_op jit(solution)/shard_map/ppermute | solution.py:31
  547.8 126.1 %copy-start.3 = (f32[1024,512]{1,0:T(8,128)S(1)}, f32[1024,512]{1,0:T(8,128)}, u32[]{:S(2)}) copy-start(f32[1024,512]{1,0:T(8,128)} %param.6) | copy-start | bytes 6291460
  (8 other events, 43.1 us)
Sparse Core Ops, SparseCore 0:
  10.3 121.2 all-gather.11
  133.5 54.6 all-gather.9
  190.1 55.8 all-gather.13
  259.4 80.7 all-gather.17
  341.9 54.3 all-gather.15
  397.7 81.3 all-gather.25
  481.0 54.3 all-gather.23
  536.9 80.7 all-gather.19
  619.6 54.3 all-gather.21
